TPU v7x, 128 devices: a whole 4x4x4 slice. The times are simulated.
128 devices in a mesh: grp: 4 (over z_lo, core), dp: 32 (over z_hi, y, x).
Axes of the slice: x: 4, y: 4, z: 4 (z_hi: 2, z_lo: 2; z = z_hi * 2 + z_lo), core: 2. Of those that a mesh axis runs over, the one named last changes fastest.
Arguments:
- activations: bfloat16 [262144, 1280], P(('grp', 'dp')), may hold values from -6 to 6
- cotangent: bfloat16 [262144, 1280], P(('grp', 'dp')), may hold values from -0.01171875 to 0.01171875
- carried_error: float32 [128, 1280, 1280], P(('grp', 'dp')), may hold values from -6 to 6
- owner_error: float32 [1280, 1280], P(('grp', 'dp')), may hold values from -6 to 6
Outputs:
- update: float32 [1280, 1280], replicated
All inputs are finite; a program needn't handle non-finite values.
Results may differ from a plain program's by a relative error of at most 0.012.
Values may be sent and summed in bfloat16 or wider, within the bound.
A program may use at most 128 MiB of HBM per device.

v0:
```python
import jax
import jax.numpy as jnp
from jax import lax
from jax.sharding import PartitionSpec as P

D = 1280
BLOCK = 128


def quantize(values):
    blocks = values.reshape(values.shape[:-1] + (values.shape[-1] // BLOCK, BLOCK))
    largest = jnp.max(jnp.abs(blocks), axis=-1)
    scales = ((largest + 1e-06) / 127.0).astype(jnp.bfloat16)
    levels = (blocks / scales.astype(jnp.float32)[..., None]).astype(jnp.bfloat16)
    return (levels.reshape(values.shape), scales)


def dequantize(levels, scales):
    blocks = levels.reshape(levels.shape[:-1] + (levels.shape[-1] // BLOCK, BLOCK)).astype(
        jnp.float32
    )
    return (blocks * scales.astype(jnp.float32)[..., None]).reshape(levels.shape)


def on_device(activations, cotangent, carried_error, owner_error):
    gradient = lax.dot_general(
        activations, cotangent, (((0,), (0,)), ((), ())), preferred_element_type=jnp.float32
    )
    own = dequantize(*quantize(gradient + carried_error[0]))
    rows = owner_error.shape[0]
    start = rows * (lax.axis_index("grp") * lax.axis_size("dp") + lax.axis_index("dp"))
    mine = lax.dynamic_slice_in_dim(own, start, rows, 0) + owner_error
    own = lax.dynamic_update_slice_in_dim(own, mine, start, 0)
    summed = lax.psum(own.astype(jnp.bfloat16), ("grp", "dp")).astype(jnp.float32)
    return dequantize(*quantize(summed))


def solution(mesh):
    return jax.shard_map(
        on_device,
        mesh=mesh,
        in_specs=(
            P(("grp", "dp"), None),
            P(("grp", "dp"), None),
            P(("grp", "dp"), None, None),
            P(("grp", "dp"), None),
        ),
        out_specs=P(),
        check_vma=False,
    )
```

profile of v0, /device:TPU:1, one launch (start us, length us, event | category | flops | bytes accessed | tf_op | source)
XLA Modules:
  0.0 257.3 jit_solution(2272758399839218393)
XLA Ops:
  6.5 0.0 all-reduce.2.cloned.1.call-start
  6.5 14.4 %fusion.3 = (f32[1280,1280]{1,0:T(8,128)}, f32[1280,1280]{1,0:T(8,128)}) fusion(f32[1,1280,1280]{2,1,0:T(8,128)} %param.6, bf16[2048,1280]{1,0:T(8,128)(2,1)} %param.4, bf16[2048,1280]{1,0:T(8,128)(2,1)} %param.5), kind=kOutput, calls=%fused_computation.12 | convolution fusion | flops 6714163200 | bytes 30146560 | tf_op jit(solution)/shard_map/dot_general | solution.py:26
  21.0 8.2 %copy.5 = f32[1280,1280]{0,1:T(8,128)} copy(f32[1280,1280]{1,0:T(8,128)} %get-tuple-element.5) | data formatting | bytes 13107200 | tf_op jit(solution)/shard_map/abs | solution.py:12
  29.1 3.3 %reduce_max.18 = f32[1280,10]{0,1:T(8,128)S(1)} reduce(f32[1280,10,128]{0,2,1:T(8,128)} %bitcast.9, f32[]{:T(128)} %constant.5.clone.1), dimensions={2}, to_apply=%region_0.0 | reduce | flops 1625600 | bytes 6604804 | tf_op jit(solution)/shard_map/reduce_max | solution.py:12
  32.4 3.3 %div.29 = f32[1280,10,128]{0,2,1:T(8,128)} broadcast(f32[1280,10]{0,1:T(8,128)S(1)} %fusion.1), dimensions={0,1} | broadcast | bytes 6604800 | tf_op jit(solution)/shard_map/div | solution.py:14
  35.7 8.2 %copy.6 = f32[1280,1280]{1,0:T(8,128)} copy(f32[1280,1280]{0,1:T(8,128)} %bitcast.10) | data formatting | bytes 13107200 | tf_op jit(solution)/shard_map/div | solution.py:14
  43.9 0.0 copy-start.1
  43.9 8.4 %convert_multiply_fusion.1 = f32[1280,1280]{1,0:T(8,128)} fusion(f32[1280,1280]{1,0:T(8,128)} %copy.6, f32[1280,1280]{1,0:T(8,128)} %get-tuple-element.6), kind=kLoop, calls=%fused_computation.5 | loop fusion | flops 6553600 | bytes 19660800 | tf_op jit(solution)/shard_map/mul | solution.py:22
  52.3 0.0 copy-done.1
  52.3 0.9 dynamic-slice_add_fusion
  53.2 1.6 dynamic_update_slice.3
  54.8 4.9 %convert_element_type.56 = bf16[1280,1280]{1,0:T(8,128)(2,1)} convert(f32[1280,1280]{1,0:T(8,128)} %dynamic_update_slice.3) | non-fusion elementwise | flops 1638400 | bytes 9830400 | tf_op jit(solution)/shard_map/convert_element_type | solution.py:34
  59.7 0.0 all-reduce.2.cloned.1.call-update
  59.7 155.8 %all-reduce.2.cloned.1.call-done = bf16[1280,1280]{1,0:T(8,128)(2,1)} async-done(((bf16[1280,1280]{1,0:T(8,128)(2,1)}), bf16[1280,1280]{1,0:T(8,128)(2,1)}) %all-reduce.2.cloned.1.call-update) | async-done | bytes 3276816 | tf_op jit(solution)/shard_map/psum | solution.py:34
  215.6 5.3 %convert_abs_fusion = f32[1280,1280]{1,0:T(8,128)} fusion(bf16[1280,1280]{1,0:T(8,128)(2,1)} %all-reduce.2.cloned.1.call-done), kind=kLoop, calls=%fused_computation.2 | loop fusion | flops 3276800 | bytes 9830400 | tf_op jit(solution)/shard_map/abs | solution.py:12
  220.9 8.2 %copy.8 = f32[1280,1280]{0,1:T(8,128)} copy(f32[1280,1280]{1,0:T(8,128)} %convert_abs_fusion) | data formatting | bytes 13107200 | tf_op jit(solution)/shard_map/abs | solution.py:12
  229.0 3.3 %reduce_max.19 = f32[1280,10]{0,1:T(8,128)S(1)} reduce(f32[1280,10,128]{0,2,1:T(8,128)} %bitcast.8, f32[]{:T(128)} %constant.5.clone.1), dimensions={2}, to_apply=%region_2.0 | reduce | flops 1625600 | bytes 6604804 | tf_op jit(solution)/shard_map/reduce_max | solution.py:12
  232.3 3.3 %div.33 = f32[1280,10,128]{0,2,1:T(8,128)} broadcast(f32[1280,10]{0,1:T(8,128)S(1)} %fusion.2), dimensions={0,1} | broadcast | bytes 6604800 | tf_op jit(solution)/shard_map/div | solution.py:14
  235.6 0.0 copy-start
  235.6 8.3 %copy.9 = f32[1280,1280]{1,0:T(8,128)} copy(f32[1280,1280]{0,1:T(8,128)} %bitcast.11) | data formatting | bytes 13107200 | tf_op jit(solution)/shard_map/div | solution.py:14
  243.9 0.0 copy-done
  243.9 6.5 %convert_multiply_fusion = f32[1280,1280]{1,0:T(8,128)} fusion(f32[1280,1280]{1,0:T(8,128)} %copy.9, bf16[1280,1280]{1,0:T(8,128)(2,1)S(1)} %copy-done), kind=kLoop, calls=%fused_computation.4 | loop fusion | flops 8192000 | bytes 16384000 | tf_op jit(solution)/shard_map/mul | solution.py:22
  (2 shorter events, 0.0 us)
Async XLA Ops:
  6.5 209.0 %all-reduce.2.cloned.1.call-start = ((), (), s32[]{:S(2)}) async-start(), calls=%async_computation | async-start | bytes 6553600 | tf_op jit(solution)/shard_map/psum | solution.py:34
  43.9 8.4 %copy-start.1 = (f32[10,1280]{1,0:T(8,128)S(1)}, f32[10,1280]{1,0:T(8,128)}, u32[]{:S(2)}) copy-start(f32[10,1280]{1,0:T(8,128)} %param.7) | copy-start | bytes 153604
  235.6 8.3 %copy-start = (bf16[1280,1280]{1,0:T(8,128)(2,1)S(1)}, bf16[1280,1280]{1,0:T(8,128)(2,1)}, u32[]{:S(2)}) copy-start(bf16[1280,1280]{1,0:T(8,128)(2,1)} %all-reduce.2.cloned.1.call-done) | copy-start | bytes 9830404
Sparse Core Ops, SparseCore 0:
  59.9 155.6 all-reduce.1
where the time goes:
time: 258 us; the launch traced here: 257 us
  waiting for transfers between devices  156 us (60%)
  local copies, waits for them, and re-layouts  41 us (16%)
  other arithmetic  32.6 us (13%)
  matrix products  14.4 us (6%)
  between operations  13.4 us (5%)
    psum x1, waiting for transfers between devices, on_device(): lax.psum(own.astype(jnp.bfloat16), ('grp', 'dp')).astype(jnp.float32)  156 us
    div x4, local copies, waits for them, and re-layouts, quantize(): blocks / scales.astype(jnp.float32)[..., None]  23.1 us
    abs x2, local copies, waits for them, and re-layouts, quantize(): largest = jnp.max(jnp.abs(blocks), axis=-1)  16.3 us
    mul x2, other arithmetic, dequantize(): blocks * scales.astype(jnp.float32)[..., None]  14.9 us
    dot_general x1, matrix products, on_device(): lax.dot_general(activations, cotangent, (((0,), (0,)), ((), ())), preferr...  14.4 us
    reduce_max x2, other arithmetic, quantize(): largest = jnp.max(jnp.abs(blocks), axis=-1)  6.56 us
    abs x1, other arithmetic, quantize(): largest = jnp.max(jnp.abs(blocks), axis=-1)  5.29 us
  transfers between devices with their start and end apart: 1, of which 1 were waited for; matrix products, arithmetic and copies ran while one was open for 0% of the time, Pallas kernels for 0%

commit v1 on v0

--- a/solution.py
+++ b/solution.py
@@ -31,7 +31,7 @@
     start = rows * (lax.axis_index("grp") * lax.axis_size("dp") + lax.axis_index("dp"))
     mine = lax.dynamic_slice_in_dim(own, start, rows, 0) + owner_error
     own = lax.dynamic_update_slice_in_dim(own, mine, start, 0)
-    summed = lax.psum(own.astype(jnp.bfloat16), ("grp", "dp")).astype(jnp.float32)
+    summed = lax.psum(lax.psum(own.astype(jnp.bfloat16), "dp"), "grp").astype(jnp.float32)
     return dequantize(*quantize(summed))
 
 

time: 258 us -> 545 us (2.11)
  waiting for transfers between devices: 156 us -> 443 us
    psum x1 -> x2, waiting for transfers between devices: 156 us -> 443 us  [the longest x1 344 us: on_device(): lax.psum(own.astype(jnp.bfloat16), 'dp')]
  transfers between devices with their start and end apart: 1 -> 2, of which waited for: 1 -> 2; matrix products, arithmetic and copies ran while one was open for 0% -> 0% of each run, Pallas kernels for 0% -> 0%
where the time goes in v1:
time: 545 us; the launch traced here: 544 us
  waiting for transfers between devices  443 us (81%)
  local copies, waits for them, and re-layouts  41 us (8%)
  other arithmetic  32.6 us (6%)
  matrix products  14.4 us (3%)
  between operations  13.4 us (2%)
    psum x1, waiting for transfers between devices, on_device(): lax.psum(own.astype(jnp.bfloat16), 'dp')  344 us
    psum x1, waiting for transfers between devices, on_device(): lax.psum(lax.psum(own.astype(jnp.bfloat16), 'dp'), 'grp')  98.5 us
    div x4, local copies, waits for them, and re-layouts, quantize(): blocks / scales.astype(jnp.float32)[..., None]  23.1 us
    abs x2, local copies, waits for them, and re-layouts, quantize(): largest = jnp.max(jnp.abs(blocks), axis=-1)  16.3 us
    mul x2, other arithmetic, dequantize(): blocks * scales.astype(jnp.float32)[..., None]  14.9 us
    dot_general x1, matrix products, on_device(): lax.dot_general(activations, cotangent, (((0,), (0,)), ((), ())), preferr...  14.4 us
  transfers between devices with their start and end apart: 2, of which 2 were waited for; matrix products, arithmetic and copies ran while one was open for 0% of the time, Pallas kernels for 0%

profile of v1, /device:TPU:1, one launch (start us, length us, event | category | flops | bytes accessed | tf_op | source)
XLA Modules:
  0.0 544.2 jit_solution(7546840034025601397)
XLA Ops:
  6.5 0.0 all-reduce.3.cloned.1.call-start
  6.5 14.4 %fusion.3 = (f32[1280,1280]{1,0:T(8,128)}, f32[1280,1280]{1,0:T(8,128)}) fusion(f32[1,1280,1280]{2,1,0:T(8,128)} %param.6, bf16[2048,1280]{1,0:T(8,128)(2,1)} %param.4, bf16[2048,1280]{1,0:T(8,128)(2,1)} %param.5), kind=kOutput, calls=%fused_computation.12 | convolution fusion | flops 6714163200 | bytes 30146560 | tf_op jit(solution)/shard_map/dot_general | solution.py:26
  21.0 8.2 %copy.5 = f32[1280,1280]{0,1:T(8,128)} copy(f32[1280,1280]{1,0:T(8,128)} %get-tuple-element.5) | data formatting | bytes 13107200 | tf_op jit(solution)/shard_map/abs | solution.py:12
  29.1 3.3 reduce_max.18
  32.4 3.3 div.29
  35.7 8.2 %copy.6 = f32[1280,1280]{1,0:T(8,128)} copy(f32[1280,1280]{0,1:T(8,128)} %bitcast.10) | data formatting | bytes 13107200 | tf_op jit(solution)/shard_map/div | solution.py:14
  43.9 0.0 copy-start.1
  43.9 8.4 %convert_multiply_fusion.1 = f32[1280,1280]{1,0:T(8,128)} fusion(f32[1280,1280]{1,0:T(8,128)} %copy.6, f32[1280,1280]{1,0:T(8,128)} %get-tuple-element.6), kind=kLoop, calls=%fused_computation.5 | loop fusion | flops 6553600 | bytes 19660800 | tf_op jit(solution)/shard_map/mul | solution.py:22
  52.3 0.0 copy-done.1
  52.3 0.9 dynamic-slice_add_fusion
  53.2 1.6 dynamic_update_slice.3
  54.8 4.9 convert_element_type.56
  59.7 0.0 all-reduce.3.cloned.1.call-update
  59.8 0.0 all-reduce.5.cloned.1.call-start
  59.8 344.2 %all-reduce.3.cloned.1.call-done = bf16[1280,1280]{1,0:T(8,128)(2,1)} async-done(((bf16[1280,1280]{1,0:T(8,128)(2,1)}), bf16[1280,1280]{1,0:T(8,128)(2,1)}) %all-reduce.3.cloned.1.call-update) | async-done | bytes 3276816 | tf_op jit(solution)/shard_map/psum | solution.py:34
  404.0 0.0 all-reduce.5.cloned.1.call-update
  404.0 98.5 %all-reduce.5.cloned.1.call-done = bf16[1280,1280]{1,0:T(8,128)(2,1)} async-done(((bf16[1280,1280]{1,0:T(8,128)(2,1)}), bf16[1280,1280]{1,0:T(8,128)(2,1)}) %all-reduce.5.cloned.1.call-update) | async-done | bytes 3276816 | tf_op jit(solution)/shard_map/psum | solution.py:34
  502.5 5.3 convert_abs_fusion
  507.8 8.2 %copy.8 = f32[1280,1280]{0,1:T(8,128)} copy(f32[1280,1280]{1,0:T(8,128)} %convert_abs_fusion) | data formatting | bytes 13107200 | tf_op jit(solution)/shard_map/abs | solution.py:12
  516.0 3.3 reduce_max.19
  519.3 3.3 div.33
  522.6 0.0 copy-start
  522.6 8.3 %copy.9 = f32[1280,1280]{1,0:T(8,128)} copy(f32[1280,1280]{0,1:T(8,128)} %bitcast.11) | data formatting | bytes 13107200 | tf_op jit(solution)/shard_map/div | solution.py:14
  530.9 0.0 copy-done
  530.9 6.5 %convert_multiply_fusion = f32[1280,1280]{1,0:T(8,128)} fusion(f32[1280,1280]{1,0:T(8,128)} %copy.9, bf16[1280,1280]{1,0:T(8,128)(2,1)S(1)} %copy-done), kind=kLoop, calls=%fused_computation.4 | loop fusion | flops 8192000 | bytes 16384000 | tf_op jit(solution)/shard_map/mul | solution.py:22
  (2 shorter events, 0.0 us)
Async XLA Ops:
  6.5 397.5 %all-reduce.3.cloned.1.call-start = ((), (), s32[]{:S(2)}) async-start(), calls=%async_computation | async-start | bytes 6553600 | tf_op jit(solution)/shard_map/psum | solution.py:34
  43.9 8.4 %copy-start.1 = (f32[10,1280]{1,0:T(8,128)S(1)}, f32[10,1280]{1,0:T(8,128)}, u32[]{:S(2)}) copy-start(f32[10,1280]{1,0:T(8,128)} %param.7) | copy-start | bytes 153604
  59.8 442.7 %all-reduce.5.cloned.1.call-start = ((), (), s32[]{:S(2)}) async-start(), calls=%async_computation.1 | async-start | bytes 6553600 | tf_op jit(solution)/shard_map/psum | solution.py:34
  522.6 8.3 %copy-start = (bf16[1280,1280]{1,0:T(8,128)(2,1)S(1)}, bf16[1280,1280]{1,0:T(8,128)(2,1)}, u32[]{:S(2)}) copy-start(bf16[1280,1280]{1,0:T(8,128)(2,1)} %all-reduce.5.cloned.1.call-done) | copy-start | bytes 9830404
Sparse Core Ops, SparseCore 0:
  59.9 344.0 all-reduce.2
  406.6 95.9 all-reduce.4
